TPU v7x, 32 devices: a whole 2x2x4 slice. The times are simulated.
32 devices in a mesh: lat: 4 (over x, core), lon: 8 (over z, y).
Axes of the slice: x: 2, y: 2, z: 4, core: 2. Of those that a mesh axis runs over, the one named last changes fastest.
Arguments:
- tracers: bfloat16 [256, 1024, 32, 4], P('lat', 'lon'), may hold values from 0 to 2
- weights: bfloat16 [256, 8, 8, 128, 128], P('lat', 'lon'), may hold values from -1 to 1, as said below
- source_row: int32 [256, 8, 8], P('lat', 'lon'), may hold values from 0 to 255, as said below
- source_block: int32 [256, 8, 8], P('lat', 'lon'), may hold values from 0 to 7, as said below
- slot_count: int32 [256, 8], P('lat', 'lon'), may hold values from 1 to 8, as said below
Outputs:
- advected_fixed: float32 [256, 1024, 32, 4], P('lat', 'lon')
Inputs may be any that keep to these rules, and one draw needn't show every extreme that they name: source_row differs from the target tile's own row by at most 4 and lies within the grid. source_block lies at cyclic distance at most 2 from the target tile's own index along the row, except for target tiles of the first and the last latitude row, where it may reach 3; the allowed distance grows from 1 at the equator towards the poles; in the two outermost rows slot 0 reaches exactly 3 sectors ahead on even tiles and 3 sectors behind on odd tiles. slot_count grows from 1 or 2 at the equator to 8 at the two outermost rows. weights are of either sign; for each target tile the weights of each target cell over the used slots and all source cells sum (before rounding to bfloat16) to one value of that tile between 0.9 and 1.05.
All inputs are finite; a program needn't handle non-finite values.
Results may differ from a plain program's by a relative error of at most 0.0003.
Values may be sent and summed in bfloat16 or wider, within the bound.
A program may use at most 192 MiB of HBM per device.

v0:
```python
import math

import jax
import jax.numpy as jnp
from jax import lax
from jax.sharding import PartitionSpec as P

RLAT = 4
REACH = 3


def extended(value, sides, width):
    for axis, dim in sides:
        size, length = (lax.axis_size(axis), value.shape[dim])
        up = [(i, (i + 1) % size) for i in range(size - 1)]
        down = [(j, i) for i, j in up]
        last = lax.slice_in_dim(value, length - width, length, axis=dim)
        leading = lax.slice_in_dim(value, 0, width, axis=dim)
        before = lax.ppermute(last, axis, up)
        after = lax.ppermute(leading, axis, down)
        value = jnp.concatenate([before, value, after], axis=dim)
    return value


def shifted(value, axis, by):
    length = lax.axis_size(axis)
    return lax.ppermute(value, axis, [(i, (i + by) % length) for i in range(length)])


def latitude_area(total_rows, first_row, count_rows):
    rows_all = jnp.arange(count_rows, dtype=jnp.int32) + first_row
    angle = -0.5 * math.pi + (rows_all.astype(jnp.float32) + 0.5) * (math.pi / total_rows)
    return jnp.cos(angle)


def local(tracers, weights, source_row, source_block, slot_count):
    rows_dev, tile_width, levels, tracer_kinds = tracers.shape
    channels = levels * tracer_kinds
    lat_count = lax.axis_size("lat")
    lon_count = lax.axis_size("lon")
    lat_index = lax.axis_index("lat")
    lon_index = lax.axis_index("lon")
    field = tracers.reshape(rows_dev, tile_width, channels)
    total_rows = rows_dev * lat_count
    area = latitude_area(total_rows, lat_index * rows_dev, rows_dev)
    total_area = tile_width * lon_count * jnp.sum(latitude_area(total_rows, 0, total_rows))
    mass_old = jnp.sum(area[:, None, None] * field, axis=(0, 1))
    padded = extended(field, (("lat", 0),), RLAT)
    local_row = source_row[:, 0, :] - (lat_index * rows_dev - RLAT)
    wanted = source_block[:, 0, :]
    slots_max = source_row.shape[2]
    relative = (wanted - lon_index + REACH) % lon_count - REACH
    near_list = []
    for distance in range(-(REACH - 1), REACH):
        if distance == 0:
            near_list.append(padded)
        else:
            near_list.append(shifted(padded, "lon", -distance))
    near_stack = jnp.stack(near_list, axis=1)
    near_pick = near_stack[local_row, jnp.clip(relative + REACH - 1, 0, 2 * REACH - 2)]
    polar_slab = jnp.concatenate(
        [padded[RLAT : 2 * RLAT + 1], padded[rows_dev - 1 : rows_dev + RLAT]], axis=0
    )
    far_list = [shifted(polar_slab, "lon", -distance) for distance in (-REACH, REACH)]
    upper = (jnp.arange(rows_dev, dtype=jnp.int32) < rows_dev // 2)[:, None]
    far_row = jnp.where(upper, local_row - RLAT, local_row - (rows_dev - 1) + RLAT + 1)
    far_row = jnp.clip(far_row, 0, 2 * RLAT + 1)
    far_stack = jnp.stack(far_list, axis=1)
    far_pick = far_stack[
        jnp.clip(far_row, 0, far_stack.shape[0] - 1), (relative > 0).astype(jnp.int32)
    ]
    active = jnp.arange(slots_max, dtype=jnp.int32)[None, :] < slot_count
    is_far = jnp.abs(relative) == REACH
    picked = jnp.where(
        (active & is_far)[:, :, None, None],
        far_pick,
        jnp.where(active[:, :, None, None], near_pick, jnp.zeros((), near_pick.dtype)),
    )
    advected = jnp.einsum(
        "tkij,tkjc->tic", weights[:, 0], picked, preferred_element_type=jnp.float32
    )
    mass_new = jnp.sum(area[:, None, None] * advected, axis=(0, 1))
    summed_old, summed_new = lax.psum((mass_old, mass_new), ("lat", "lon"))
    fixed = advected + (summed_old - summed_new) / total_area
    return fixed.reshape(rows_dev, tile_width, levels, tracer_kinds)


def solution(mesh):
    return jax.shard_map(
        local,
        mesh=mesh,
        in_specs=(
            P("lat", "lon", None, None),
            P("lat", "lon", None, None, None),
            P("lat", "lon", None),
            P("lat", "lon", None),
            P("lat", "lon"),
        ),
        out_specs=P("lat", "lon", None, None),
        check_vma=False,
    )
```

profile of v0, /device:TPU:0, one launch (start us, length us, event | category | flops | bytes accessed | tf_op | source)
XLA Modules:
  0.0 299.1 jit_solution(15914645323149280018)
XLA Ops:
  0.0 0.0 copy-start
  0.0 0.0 copy-start.2
  0.0 0.0 copy-start.4
  0.0 0.0 copy-start.3
  0.0 1.2 fusion.28
  1.2 2.4 collective-permute-start.2
  3.6 1.3 collective-permute-start.3
  4.9 0.0 collective-permute-done.2
  5.0 4.0 %collective-permute-done.3 = bf16[4,128,128]{1,2,0:T(8,128)(2,1)S(1)} collective-permute-done((bf16[4,128,128]{1,2,0:T(8,128)(2,1)S(1)}, bf16[4,128,128]{1,2,0:T(8,128)(2,1)S(1)}, u32[]{:S(2)}, u32[]{:S(2)}) %collective-permute-start.3) | collective-permute-done | bytes 131104 | tf_op jit(solution)/shard_map/ppermute | solution.py:20
  9.0 3.3 %pad_maximum_fusion = bf16[72,128,128]{1,2,0:T(8,128)(2,1)} fusion(bf16[4,128,128]{1,2,0:T(8,128)(2,1)S(1)} %collective-permute-done.3, bf16[64,128,128]{1,2,0:T(8,128)(2,1)} %bitcast.64, bf16[4,128,128]{1,2,0:T(8,128)(2,1)S(1)} %collective-permute-done.2), kind=kLoop, calls=%fused_computation.13 | loop fusion | flops 2359296 | bytes 4718592 | tf_op jit(solution)/shard_map/concatenate | solution.py:21
  12.3 1.6 collective-permute-start.4
  13.8 1.5 collective-permute-start.5
  15.4 3.2 %collective-permute-start.6 = (bf16[72,128,128]{1,2,0:T(8,128)(2,1)}, bf16[72,128,128]{1,2,0:T(8,128)(2,1)}, u32[]{:S(2)}, u32[]{:S(2)}) collective-permute-start(bf16[72,128,128]{1,2,0:T(8,128)(2,1)} %pad_maximum_fusion), channel_id=1, source_target_pairs={{0,7},{1,0},{2,1},{3,2},{4,3},{5,4},{6,5},{7,6},{8,15},{9,8},{10,9... | collective-permute-start | bytes 7077896 | tf_op jit(solution)/shard_map/ppermute | solution.py:27
  18.6 0.0 copy-done
  18.6 0.1 fusion.29
  18.7 0.5 collective-permute-start.7
  19.2 0.1 collective-permute-start
  19.3 0.0 copy-done.2
  19.3 0.0 copy-done.4
  19.4 0.0 copy-done.3
  19.4 165.0 %collective-permute-done = bf16[10,128,128]{1,2,0:T(8,128)(2,1)S(1)} collective-permute-done((bf16[10,128,128]{1,2,0:T(8,128)(2,1)S(1)}, bf16[10,128,128]{1,2,0:T(8,128)(2,1)S(1)}, u32[]{:S(2)}, u32[]{:S(2)}) %collective-permute-start) | collective-permute-done | bytes 327712 | tf_op jit(solution)/shard_map/ppermute | solution.py:27
  184.4 0.0 collective-permute-start.1
  184.5 0.1 copy.11
  184.6 0.1 reshape.258
  184.6 0.1 copy.9
  184.7 0.1 reshape.252
  184.8 0.1 copy.10
  184.9 0.1 copy.8
  185.0 1.4 multiply_reduce_fusion
  186.4 0.1 reduce_sum.30
  186.5 0.6 cosine_reduce_fusion
  187.7 7.3 %collective-permute-done.1 = bf16[10,128,128]{1,2,0:T(8,128)(2,1)S(1)} collective-permute-done((bf16[10,128,128]{1,2,0:T(8,128)(2,1)S(1)}, bf16[10,128,128]{1,2,0:T(8,128)(2,1)S(1)}, u32[]{:S(2)}, u32[]{:S(2)}) %collective-permute-start.1) | collective-permute-done | bytes 327712 | tf_op jit(solution)/shard_map/ppermute | solution.py:27
  195.0 0.0 copy-start.1
  195.1 0.7 copy-done.1
  195.8 1.0 pad_maximum_fusion.1
  196.8 10.8 %gather_fusion = bf16[512,128,128]{1,2,0:T(8,128)(2,1)} fusion(bf16[10,2,128,128]{2,3,0,1:T(8,128)(2,1)S(1)} %pad_maximum_fusion.1, s32[512]{0:T(512)S(1)} %reshape.252), kind=kCustom, calls=%fused_computation | custom fusion | bytes 33558528 | tf_op jit(solution)/shard_map/gather | solution.py:69
  207.6 0.0 collective-permute-done.4
  207.6 3.3 %bitcast_dynamic-update-slice_fusion.4 = bf16[72,5,128,128]{2,3,0,1:T(8,128)(2,1)} fusion(bf16[72,128,128]{1,2,0:T(8,128)(2,1)} %collective-permute-done.4), kind=kLoop, calls=%fused_computation.18 | loop fusion | bytes 4718592
  210.9 0.0 collective-permute-done.5
  210.9 3.4 %bitcast_dynamic-update-slice_fusion.3 = bf16[72,5,128,128]{2,3,0,1:T(8,128)(2,1)} fusion(bf16[72,5,128,128]{2,3,0,1:T(8,128)(2,1)} %bitcast_dynamic-update-slice_fusion.4, bf16[72,128,128]{1,2,0:T(8,128)(2,1)} %collective-permute-done.5), kind=kLoop, calls=%fused_computation.17 | loop fusion | bytes 4718592
  214.3 1.7 bitcast_dynamic-update-slice_fusion.2
  216.0 0.0 collective-permute-done.6
  216.1 3.4 %bitcast_dynamic-update-slice_fusion.1 = bf16[72,5,128,128]{2,3,0,1:T(8,128)(2,1)} fusion(bf16[72,5,128,128]{2,3,0,1:T(8,128)(2,1)} %bitcast_dynamic-update-slice_fusion.2, bf16[72,128,128]{1,2,0:T(8,128)(2,1)} %collective-permute-done.6), kind=kLoop, calls=%fused_computation.15 | loop fusion | bytes 4718592
  219.4 0.0 collective-permute-done.7
  219.4 3.4 %bitcast_dynamic-update-slice_fusion = bf16[72,5,128,128]{2,3,0,1:T(8,128)(2,1)} fusion(bf16[72,5,128,128]{2,3,0,1:T(8,128)(2,1)} %bitcast_dynamic-update-slice_fusion.1, bf16[72,128,128]{1,2,0:T(8,128)(2,1)} %collective-permute-done.7), kind=kLoop, calls=%fused_computation.14 | loop fusion | bytes 4718592 | tf_op jit(solution)/shard_map/stack | solution.py:59
  222.8 15.2 %gather_fusion.1 = bf16[512,128,128]{1,2,0:T(8,128)(2,1)} fusion(bf16[72,5,128,128]{2,3,0,1:T(8,128)(2,1)} %bitcast_dynamic-update-slice_fusion, s32[512]{0:T(512)S(1)} %reshape.258), kind=kCustom, calls=%fused_computation.1 | custom fusion | bytes 33558528 | tf_op jit(solution)/shard_map/gather | solution.py:60
  238.0 19.4 %fusion.7 = (f32[128]{0:T(128)S(1)}, f32[64,128,128,1]{2,1,3,0:T(8,128)}) fusion(f32[64]{0:T(128)S(1)} %add_cosine_fusion, bf16[64,1,8,128,128]{4,3,2,1,0:T(8,128)(2,1)} %param.6, bf16[64,8,128,128]{2,3,1,0:T(8,128)(2,1)} %bitcast.66, bf16[64,8,128,128]{2,3,1,0:T(8,128)(2,1)} %bitcast.67, pred[64,8]{1,0:T(8,128)(4,1)S(1)} %copy.10, pred[64,8]{1,0:T(8,128)(4,1)S(1)} %copy.8), kind=kOutput, calls=%fused_computation.11 | convolution fusion | flops 2166358016 | bytes 54527744 | tf_op jit(solution)/shard_map/tkij,tkjc->tic/dot_general | solution.py:79
  257.4 36.8 %all-reduce = (f32[128]{0:T(128)S(1)}, f32[128]{0:T(128)S(1)}) all-reduce(f32[128]{0:T(128)S(1)} %reduce_sum.30, f32[128]{0:T(128)S(1)} %get-tuple-element.15), channel_id=1, replica_groups=mesh['lat'=4,'lon'=8] {'lat','lon'}, use_global_device_ids=true, to_apply=%region_1.0 | all-reduce | flops 256 | bytes 2048 | tf_op jit(solution)/shard_map/psum | solution.py:83
  294.2 4.9 %bitcast_add_fusion = f32[64,128,128]{2,1,0:T(8,128)} fusion(f32[64,128,128,1]{2,1,3,0:T(8,128)} %get-tuple-element.16, f32[128]{0:T(128)S(1)} %subtract_divide_fusion), kind=kLoop, calls=%fused_computation.9 | loop fusion | flops 1048576 | bytes 8389120 | tf_op jit(solution)/shard_map/add | solution.py:84
  (6 shorter events, 0.1 us)
Async XLA Ops:
  0.0 18.6 %copy-start = (bf16[64,128,32,4]{1,3,2,0:T(4,128)(2,1)S(1)}, bf16[64,128,32,4]{1,3,2,0:T(4,128)(2,1)}, u32[]{:S(2)}) copy-start(bf16[64,128,32,4]{1,3,2,0:T(4,128)(2,1)} %param.5) | copy-start | bytes 6291460
  0.0 19.3 %copy-start.2 = (s32[64,1,8]{0,2,1:T(8,128)S(1)}, s32[64,1,8]{0,2,1:T(8,128)}, u32[]{:S(2)}) copy-start(s32[64,1,8]{0,2,1:T(8,128)} %param.8) | copy-start | bytes 6148
  0.0 19.3 %copy-start.4 = (s32[64,1]{0,1:T(1,128)S(1)}, s32[64,1]{0,1:T(1,128)}, u32[]{:S(2)}) copy-start(s32[64,1]{0,1:T(1,128)} %param.9) | copy-start | bytes 772
  0.0 19.4 %copy-start.3 = (s32[64,1,8]{0,2,1:T(8,128)S(1)}, s32[64,1,8]{0,2,1:T(8,128)}, u32[]{:S(2)}) copy-start(s32[64,1,8]{0,2,1:T(8,128)} %param.7) | copy-start | bytes 6148
  1.2 3.7 %collective-permute-start.2 = (bf16[4,128,128]{1,2,0:T(8,128)(2,1)S(1)}, bf16[4,128,128]{1,2,0:T(8,128)(2,1)S(1)}, u32[]{:S(2)}, u32[]{:S(2)}) collective-permute-start(bf16[4,128,128]{1,2,0:T(8,128)(2,1)S(1)} %bitcast.73), channel_id=1, source_target_pairs={{0,8},{8,16},{16,24},{1,9},{9,17},{17,25},{2,10},{10,18},{18,26},{... | collective-permute-start | bytes 393224 | tf_op jit(solution)/shard_map/ppermute | solution.py:19
  3.6 5.3 %collective-permute-start.3 = (bf16[4,128,128]{1,2,0:T(8,128)(2,1)S(1)}, bf16[4,128,128]{1,2,0:T(8,128)(2,1)S(1)}, u32[]{:S(2)}, u32[]{:S(2)}) collective-permute-start(bf16[4,128,128]{1,2,0:T(8,128)(2,1)S(1)} %bitcast.72), channel_id=1, source_target_pairs={{8,0},{16,8},{24,16},{9,1},{17,9},{25,17},{10,2},{18,10},{26,18},{... | collective-permute-start | bytes 393224 | tf_op jit(solution)/shard_map/ppermute | solution.py:20
  12.3 195.3 %collective-permute-start.4 = (bf16[72,128,128]{1,2,0:T(8,128)(2,1)}, bf16[72,128,128]{1,2,0:T(8,128)(2,1)}, u32[]{:S(2)}, u32[]{:S(2)}) collective-permute-start(bf16[72,128,128]{1,2,0:T(8,128)(2,1)} %pad_maximum_fusion), channel_id=1, source_target_pairs={{0,2},{1,3},{2,4},{3,5},{4,6},{5,7},{6,0},{7,1},{8,10},{9,11},{10,... | collective-permute-start | bytes 7077896 | tf_op jit(solution)/shard_map/ppermute | solution.py:27
  13.8 197.1 %collective-permute-start.5 = (bf16[72,128,128]{1,2,0:T(8,128)(2,1)}, bf16[72,128,128]{1,2,0:T(8,128)(2,1)}, u32[]{:S(2)}, u32[]{:S(2)}) collective-permute-start(bf16[72,128,128]{1,2,0:T(8,128)(2,1)} %pad_maximum_fusion), channel_id=1, source_target_pairs={{0,1},{1,2},{2,3},{3,4},{4,5},{5,6},{6,7},{7,0},{8,9},{9,10},{10,1... | collective-permute-start | bytes 7077896 | tf_op jit(solution)/shard_map/ppermute | solution.py:27
  15.4 200.7 %collective-permute-start.6 = (bf16[72,128,128]{1,2,0:T(8,128)(2,1)}, bf16[72,128,128]{1,2,0:T(8,128)(2,1)}, u32[]{:S(2)}, u32[]{:S(2)}) collective-permute-start(bf16[72,128,128]{1,2,0:T(8,128)(2,1)} %pad_maximum_fusion), channel_id=1, source_target_pairs={{0,7},{1,0},{2,1},{3,2},{4,3},{5,4},{6,5},{7,6},{8,15},{9,8},{10,9... | collective-permute-start | bytes 7077896 | tf_op jit(solution)/shard_map/ppermute | solution.py:27
  18.7 200.7 %collective-permute-start.7 = (bf16[72,128,128]{1,2,0:T(8,128)(2,1)}, bf16[72,128,128]{1,2,0:T(8,128)(2,1)}, u32[]{:S(2)}, u32[]{:S(2)}) collective-permute-start(bf16[72,128,128]{1,2,0:T(8,128)(2,1)} %pad_maximum_fusion), channel_id=1, source_target_pairs={{0,6},{1,7},{2,0},{3,1},{4,2},{5,3},{6,4},{7,5},{8,14},{9,15},{10,... | collective-permute-start | bytes 7077896 | tf_op jit(solution)/shard_map/ppermute | solution.py:27
  19.2 165.2 %collective-permute-start = (bf16[10,128,128]{1,2,0:T(8,128)(2,1)S(1)}, bf16[10,128,128]{1,2,0:T(8,128)(2,1)S(1)}, u32[]{:S(2)}, u32[]{:S(2)}) collective-permute-start(bf16[10,128,128]{1,2,0:T(8,128)(2,1)S(1)} %pad_maximum_fusion.2), channel_id=1, source_target_pairs={{0,3},{1,4},{2,5},{3,6},{4,7},{5,0},{6,1},{7,2},{8,11},{9,12},{10,... | collective-permute-start | bytes 983048 | tf_op jit(solution)/shard_map/ppermute | solution.py:27
  184.4 10.6 %collective-permute-start.1 = (bf16[10,128,128]{1,2,0:T(8,128)(2,1)S(1)}, bf16[10,128,128]{1,2,0:T(8,128)(2,1)S(1)}, u32[]{:S(2)}, u32[]{:S(2)}) collective-permute-start(bf16[10,128,128]{1,2,0:T(8,128)(2,1)S(1)} %pad_maximum_fusion.2), channel_id=1, source_target_pairs={{0,5},{1,6},{2,7},{3,0},{4,1},{5,2},{6,3},{7,4},{8,13},{9,14},{10,... | collective-permute-start | bytes 983048 | tf_op jit(solution)/shard_map/ppermute | solution.py:27
  195.0 0.7 copy-start.1
where the time goes:
time: 300 us; the launch traced here: 299 us
  waiting for transfers between devices  176 us (59%)
  local copies, waits for them, and re-layouts  42.2 us (14%)
  blocking collectives  36.8 us (12%)
  matrix products  19.4 us (6%)
  other arithmetic  13.1 us (4%)
  starting transfers between devices  10.6 us (4%)
    ppermute x6, waiting for transfers between devices, shifted(): lax.ppermute(value, axis, [(i, (i + by) % length) for i in range(length)])  172 us
    psum x1, blocking collectives, local(): summed_old, summed_new = lax.psum((mass_old, mass_new), ('lat', 'lon'))  36.8 us
    dot_general x1, matrix products, local(): jnp.einsum('tkij,tkjc->tic', weights[:, 0], picked, preferred_element_typ...  19.4 us
    gather x1, local copies, waits for them, and re-layouts, local(): near_stack[local_row, jnp.clip(relative + REACH - 1, 0, 2 * REACH - 2)]  15.2 us
    unnamed x13, local copies, waits for them, and re-layouts  10.8 us
    gather x1, local copies, waits for them, and re-layouts, local(): far_stack[jnp.clip(far_row, 0, far_stack.shape[0] - 1), (relative > 0).as...  10.8 us
    ppermute x6, starting transfers between devices, shifted(): lax.ppermute(value, axis, [(i, (i + by) % length) for i in range(length)])  6.86 us
  transfers between devices with their start and end apart: 8, of which 3 were waited for; matrix products, arithmetic and copies ran while one was open for 9% of the time, Pallas kernels for 0%

commit v1 on v0

v1 whole, which is shorter than its diff:
```python
import functools
import math

import jax
import jax.numpy as jnp
import numpy as np
from jax import lax
from jax.experimental import pallas as pl
from jax.experimental.pallas import tpu as pltpu
from jax.sharding import PartitionSpec as P

RLAT = 4
REACH = 3
OFFSETS = tuple(d for d in range(-REACH, REACH + 1) if d != 0)
MESH = pl.DeviceIdType.MESH
ANY = pl.BlockSpec(memory_space=pl.ANY)
VMEM = pl.BlockSpec(memory_space=pltpu.VMEM)
SMEM = pl.BlockSpec(memory_space=pltpu.SMEM)


def shifted(value, axis, by):
    length = lax.axis_size(axis)
    return lax.ppermute(value, axis, [(i, (i + by) % length) for i in range(length)])


def area_table(total_rows):
    angle = -0.5 * math.pi + (np.arange(total_rows) + 0.5) * (math.pi / total_rows)
    return np.cos(angle).astype(np.float32)


def everyone(lats, lons):
    return [(a, b) for a in range(lats) for b in range(lons) if (a, b) != (0, 0)]


def send_to_all(lats, lons, mine, slots, send_sem, recv_sem):
    lat, lon = lax.axis_index("lat"), lax.axis_index("lon")
    me = lat * lons + lon
    copies = []
    for n, (a, b) in enumerate(everyone(lats, lons)):
        peer = (lax.rem(lat + a, lats), lax.rem(lon + b, lons))
        copy = pltpu.make_async_remote_copy(
            src_ref=mine,
            dst_ref=slots.at[me],
            send_sem=send_sem.at[n],
            recv_sem=recv_sem.at[n],
            device_id=peer,
            device_id_type=MESH,
        )
        copy.start()
        copies.append(copy)
    return copies


def greet(lats, lons):
    lat, lon = lax.axis_index("lat"), lax.axis_index("lon")
    barrier = pltpu.get_barrier_semaphore()
    peers = everyone(lats, lons)
    for a, b in peers:
        peer = (lax.rem(lat + a, lats), lax.rem(lon + b, lons))
        pl.semaphore_signal(barrier, inc=1, device_id=peer, device_id_type=MESH)
    pl.semaphore_wait(barrier, len(peers))


def needs_kernel(lats, lons, need, field, slots, before, after, send_sem, recv_sem, halo_send, halo_recv):
    lat, lon = lax.axis_index("lat"), lax.axis_index("lon")
    rows = field.shape[0]
    greet(lats, lons)

    def up():
        return pltpu.make_async_remote_copy(
            src_ref=field.at[pl.ds(rows - RLAT, RLAT)],
            dst_ref=before,
            send_sem=halo_send.at[0],
            recv_sem=halo_recv.at[0],
            device_id=(lax.rem(lat + 1, lats), lon),
            device_id_type=MESH,
        )

    def down():
        return pltpu.make_async_remote_copy(
            src_ref=field.at[pl.ds(0, RLAT)],
            dst_ref=after,
            send_sem=halo_send.at[1],
            recv_sem=halo_recv.at[1],
            device_id=(lax.rem(lat + lats - 1, lats), lon),
            device_id_type=MESH,
        )

    up().start()
    down().start()
    copies = send_to_all(lats, lons, need, slots, send_sem, recv_sem)
    slots[lat * lons + lon] = need[...]
    for copy in copies:
        copy.wait()
    up().wait()
    down().wait()


def share_needs(need, field, lats, lons):
    count = lats * lons
    halo = jax.ShapeDtypeStruct((RLAT,) + field.shape[1:], field.dtype)
    return pl.pallas_call(
        functools.partial(needs_kernel, lats, lons),
        out_shape=(jax.ShapeDtypeStruct((count,) + need.shape, need.dtype), halo, halo),
        in_specs=[VMEM, ANY],
        out_specs=(VMEM, ANY, ANY),
        scratch_shapes=[
            pltpu.SemaphoreType.DMA((count - 1,)),
            pltpu.SemaphoreType.DMA((count - 1,)),
            pltpu.SemaphoreType.DMA((2,)),
            pltpu.SemaphoreType.DMA((2,)),
        ],
        compiler_params=pltpu.CompilerParams(collective_id=0, has_side_effects=True),
        name="share_needs",
    )(need, field)


def total_kernel(lats, lons, part, total, slots, send_sem, recv_sem):
    greet(lats, lons)
    copies = send_to_all(lats, lons, part, slots, send_sem, recv_sem)
    slots[lax.axis_index("lat") * lons + lax.axis_index("lon")] = part[...]
    for copy in copies:
        copy.wait()
    total[...] = jnp.sum(slots[...], axis=0)


def sum_over_devices(part, lats, lons):
    count = lats * lons
    return pl.pallas_call(
        functools.partial(total_kernel, lats, lons),
        out_shape=jax.ShapeDtypeStruct(part.shape, part.dtype),
        in_specs=[VMEM],
        out_specs=VMEM,
        scratch_shapes=[
            pltpu.VMEM((count,) + part.shape, part.dtype),
            pltpu.SemaphoreType.DMA((count - 1,)),
            pltpu.SemaphoreType.DMA((count - 1,)),
        ],
        compiler_params=pltpu.CompilerParams(collective_id=1, has_side_effects=True),
        name="sum_masses",
    )(part)


def capacities(padded_rows):
    caps = {}
    for d in OFFSETS:
        if abs(d) == 1:
            caps[d] = (padded_rows * 7 // 9, padded_rows * 2 // 3)
        elif abs(d) == 2:
            caps[d] = (padded_rows * 7 // 12, 0)
        else:
            caps[d] = (RLAT + 1, 0)
    return caps


def exchange_kernel(
    lats, lons, caps, bases, lists, field, before, after, recv, padded, outgoing, load_sem, send_sem, recv_sem
):
    lat, lon = lax.axis_index("lat"), lax.axis_index("lon")
    rows = field.shape[0]
    loads = [
        pltpu.make_async_copy(before, padded.at[pl.ds(0, RLAT)], load_sem.at[0]),
        pltpu.make_async_copy(field, padded.at[pl.ds(RLAT, rows)], load_sem.at[1]),
        pltpu.make_async_copy(after, padded.at[pl.ds(RLAT + rows, RLAT)], load_sem.at[2]),
    ]
    for load in loads:
        load.start()
    barrier = pltpu.get_barrier_semaphore()
    for d in OFFSETS:
        peer = (lat, lax.rem(lon + lons - d, lons))
        pl.semaphore_signal(barrier, inc=1, device_id=peer, device_id_type=MESH)
    pl.semaphore_wait(barrier, len(OFFSETS))
    for load in loads:
        load.wait()

    polar = (lat == 0) | (lat == lats - 1)
    pieces = []
    for d in sorted(OFFSETS, key=lambda d: (abs(d), d)):
        outer, inner = caps[d]
        if inner:
            pieces.append((d, 0, inner, False))
    for d in sorted(OFFSETS, key=lambda d: (abs(d) == 1, abs(d), d)):
        outer, inner = caps[d]
        if outer > inner:
            pieces.append((d, inner, outer, True))

    def guarded(only_polar, act):
        if only_polar:
            pl.when(polar)(act)
        else:
            act()

    def copy_of(n):
        d, first, last, _ = pieces[n]
        span = pl.ds(bases[d] + first, last - first)
        return pltpu.make_async_remote_copy(
            src_ref=outgoing.at[span],
            dst_ref=recv.at[span],
            send_sem=send_sem.at[n],
            recv_sem=recv_sem.at[n],
            device_id=(lat, lax.rem(lon + lons - d, lons)),
            device_id_type=MESH,
        )

    def gather(n):
        d, first, last, _ = pieces[n]
        row = OFFSETS.index(d)

        def step(c, carry):
            outgoing[bases[d] + c] = padded[lists[row, c]]
            return carry

        lax.fori_loop(first, last, step, 0)

    for n in range(len(pieces) + 1):
        if n < len(pieces):
            guarded(pieces[n][3], functools.partial(gather, n))
        if n > 0:
            guarded(pieces[n - 1][3], lambda n=n: copy_of(n - 1).start())
    for n in range(len(pieces)):
        guarded(pieces[n][3], lambda n=n: copy_of(n).wait())


def exchange(lists, field, before, after, lats, lons, caps, bases, received):
    tile = field.shape[1:]
    padded_rows = field.shape[0] + 2 * RLAT
    count = 2 * len(OFFSETS)
    return pl.pallas_call(
        functools.partial(exchange_kernel, lats, lons, caps, bases),
        out_shape=jax.ShapeDtypeStruct((received,) + tile, field.dtype),
        in_specs=[SMEM, ANY, ANY, ANY],
        out_specs=ANY,
        scratch_shapes=[
            pltpu.VMEM((padded_rows,) + tile, field.dtype),
            pltpu.VMEM((received,) + tile, field.dtype),
            pltpu.SemaphoreType.DMA((3,)),
            pltpu.SemaphoreType.DMA((count,)),
            pltpu.SemaphoreType.DMA((count,)),
        ],
        compiler_params=pltpu.CompilerParams(collective_id=2, has_side_effects=True),
        name="exchange",
    )(lists, field, before, after)


def advect_kernel(step_rows, slots, index, counts, area, weights, field, before, after, recv, out, delta, src, gap, sem):
    g = pl.program_id(0)
    rows = field.shape[0]
    padded_rows = rows + 2 * RLAT
    received = recv.shape[0]

    @pl.when(g == 0)
    def _():
        loads = [
            pltpu.make_async_copy(before, src.at[pl.ds(0, RLAT)], sem.at[0]),
            pltpu.make_async_copy(field, src.at[pl.ds(RLAT, rows)], sem.at[1]),
            pltpu.make_async_copy(after, src.at[pl.ds(RLAT + rows, RLAT)], sem.at[2]),
            pltpu.make_async_copy(recv, src.at[pl.ds(padded_rows, received)], sem.at[3]),
        ]
        for load in loads:
            load.start()
        src[padded_rows + received] = jnp.zeros(src.shape[1:], src.dtype)
        gap[...] = jnp.zeros_like(gap)
        for load in loads:
            load.wait()

    for tt in range(step_rows):
        t = g * step_rows + tt
        used = counts[t]
        for last in range(2, slots + 2, 2):
            width = min(last, slots)

            @pl.when((used > last - 2) & (used <= last))
            def _(tt=tt, t=t, width=width):
                left = jnp.concatenate([src[index[t * slots + k]] for k in range(width)], axis=1)
                right = jnp.concatenate([weights[tt, 0, k] for k in range(width)], axis=1)
                out[tt] = lax.dot_general(
                    left, right, (((1,), (1,)), ((), ())), preferred_element_type=jnp.float32
                )

        gap[...] += area[t] * (src[RLAT + t].astype(jnp.float32) - out[tt])

    @pl.when(g == pl.num_programs(0) - 1)
    def _():
        sums = jnp.sum(gap[...].T, axis=0, keepdims=True)
        delta[...] = jnp.broadcast_to(sums, delta.shape)


def advect(index, counts, area, weights, field, before, after, recv):
    rows, channels, width = field.shape
    slots = weights.shape[2]
    step_rows = 4
    while rows % step_rows:
        step_rows -= 1
    sources = rows + 2 * RLAT + recv.shape[0] + 1
    block = (step_rows,) + weights.shape[1:]
    return pl.pallas_call(
        functools.partial(advect_kernel, step_rows, slots),
        grid=(rows // step_rows,),
        out_shape=(
            jax.ShapeDtypeStruct(field.shape, jnp.float32),
            jax.ShapeDtypeStruct((8, channels), jnp.float32),
        ),
        in_specs=[
            SMEM,
            SMEM,
            SMEM,
            pl.BlockSpec(block, lambda g: (g, 0, 0, 0, 0)),
            ANY,
            ANY,
            ANY,
            ANY,
        ],
        out_specs=(
            pl.BlockSpec((step_rows, channels, width), lambda g: (g, 0, 0)),
            pl.BlockSpec((8, channels), lambda g: (0, 0)),
        ),
        scratch_shapes=[
            pltpu.VMEM((sources, channels, width), field.dtype),
            pltpu.VMEM((channels, width), jnp.float32),
            pltpu.SemaphoreType.DMA((4,)),
        ],
        compiler_params=pltpu.CompilerParams(dimension_semantics=("arbitrary",)),
        name="advect",
    )(index, counts, area, weights, field, before, after, recv)


def dense(field, before, after, weights, local_row, relative, active, area):
    padded = jnp.concatenate([before, field, after], axis=0)
    stack = jnp.stack(
        [padded if d == 0 else shifted(padded, "lon", -d) for d in range(-REACH, REACH + 1)], axis=1
    )
    rows = jnp.clip(local_row, 0, padded.shape[0] - 1)
    picked = stack[rows, jnp.clip(relative + REACH, 0, 2 * REACH)]
    picked = jnp.where(active[:, :, None, None], picked, jnp.zeros((), picked.dtype))
    advected = jnp.einsum("tkij,tkcj->tci", weights[:, 0], picked, preferred_element_type=jnp.float32)
    gap = jnp.sum(area[:, None, None] * (field.astype(jnp.float32) - advected), axis=(0, 2))
    return advected, jnp.broadcast_to(gap[None, :], (8, gap.shape[0]))


def local(tracers, weights, source_row, source_block, slot_count):
    rows, width, levels, kinds = tracers.shape
    channels = levels * kinds
    lats, lons = lax.axis_size("lat"), lax.axis_size("lon")
    lat, lon = lax.axis_index("lat"), lax.axis_index("lon")
    field = tracers.reshape(rows, width, channels).transpose(0, 2, 1)
    slots = source_row.shape[2]
    table = area_table(rows * lats)
    total_area = float(width * lons * np.sum(table.astype(np.float64)))
    area = lax.dynamic_slice(jnp.asarray(table), (lat * rows,), (rows,))

    padded_rows = rows + 2 * RLAT
    lanes = -(-padded_rows // 128) * 128
    local_row = source_row[:, 0, :] - (lat * rows - RLAT)
    relative = (source_block[:, 0, :] - lon + REACH) % lons - REACH
    active = jnp.arange(slots, dtype=jnp.int32)[None, :] < slot_count
    remote = active & (relative != 0)
    which = jnp.where(relative < 0, relative + REACH, relative + REACH - 1)
    code = jnp.where(remote, which * lanes + local_row, -1).reshape(-1)
    hit = code[None, :] == jnp.arange(8 * lanes, dtype=jnp.int32)[:, None]
    need = jnp.any(hit, axis=1).astype(jnp.float32).reshape(8, lanes)

    needs, before, after = share_needs(need, field, lats, lons)

    caps = capacities(padded_rows)
    bases, received = {}, 0
    for d in OFFSETS:
        bases[d] = received
        received += max(caps[d])
    limit = np.zeros((lats, lons, 8), np.float32)
    for n, d in enumerate(OFFSETS):
        limit[:, :, n] = caps[d][1]
        limit[0, :, n] = limit[-1, :, n] = caps[d][0]
    over = jnp.any(jnp.sum(needs, axis=2) > jnp.asarray(limit.reshape(lats * lons, 8)))

    upto = (jnp.arange(lanes)[:, None] <= jnp.arange(lanes)[None, :]).astype(jnp.float32)

    def ranks(mask):
        return jnp.sum(mask[:, :, None] * upto[None], axis=1).astype(jnp.int32) - 1

    def fast(field, before, after, weights, needs):
        band = lax.dynamic_slice(needs, (lat * lons, 0, 0), (lons, 8, lanes))
        offsets = np.zeros((8,), np.int32)
        offsets[: len(OFFSETS)] = OFFSETS
        dest = (lon - jnp.asarray(offsets)) % lons
        chosen = jnp.arange(lons, dtype=jnp.int32)[:, None] == dest[None, :]
        wanted = jnp.sum(jnp.where(chosen[:, :, None], band, 0.0), axis=0)
        rank = jnp.where(wanted > 0, ranks(wanted), -1)
        place = jnp.arange(lanes, dtype=jnp.int32)
        match = rank[:, :, None] == place[None, None, :]
        lists = jnp.sum(jnp.where(match, place[None, :, None], 0), axis=1)
        recv = exchange(lists, field, before, after, lats, lons, caps, bases, received)
        start = np.zeros((8,), np.int32)
        start[: len(OFFSETS)] = [bases[d] + padded_rows for d in OFFSETS]
        where = (ranks(need) + jnp.asarray(start)[:, None]).reshape(-1)
        index = jnp.sum(jnp.where(hit, where[:, None], 0), axis=0)
        own = jnp.where(active, local_row, padded_rows + received).reshape(-1)
        index = jnp.where(remote.reshape(-1), index, own)
        return advect(index, slot_count[:, 0], area, weights, field, before, after, recv)

    def general(field, before, after, weights, needs):
        return dense(field, before, after, weights, local_row, relative, active, area)

    advected, delta = lax.cond(over, general, fast, field, before, after, weights, needs)
    total = sum_over_devices(delta, lats, lons)
    fixed = advected + (total[0] / total_area)[None, :, None]
    return fixed.transpose(0, 2, 1).reshape(rows, width, levels, kinds)


def solution(mesh):
    return jax.shard_map(
        local,
        mesh=mesh,
        in_specs=(
            P("lat", "lon", None, None),
            P("lat", "lon", None, None, None),
            P("lat", "lon", None),
            P("lat", "lon", None),
            P("lat", "lon"),
        ),
        out_specs=P("lat", "lon", None, None),
        check_vma=False,
    )
```

time: 300 us -> 147 us (0.49)
  waiting for transfers between devices: 176 us -> 0 us
  Pallas kernels: 0 us -> 130 us
  local copies, waits for them, and re-layouts: 42.2 us -> 2.24 us
  blocking collectives: 36.8 us -> 0 us
  matrix products: 19.4 us -> 0 us
  starting transfers between devices: 10.6 us -> 0 us
    ppermute x8 -> x0, waiting for transfers between devices: 176 us -> none  [the longest x6 172 us: shifted(): lax.ppermute(value, axis, [(i, (i + by) % length) for i in range(length)])]
    pallas_call x0 -> x4, Pallas kernels: none -> 130 us  [the longest x1 82.7 us: exchange(): pl.pallas_call(functools.partial(exchange_kernel, lats, lons, caps, bases...]
    psum x1 -> x0, blocking collectives: 36.8 us -> none  [local(): summed_old, summed_new = lax.psum((mass_old, mass_new), ('lat', 'lon'))]
    gather x2 -> x0, local copies, waits for them, and re-layouts: 26 us -> none  [the longest x1 15.2 us: local(): near_stack[local_row, jnp.clip(relative + REACH - 1, 0, 2 * REACH - 2)]]
    dot_general x1 -> x0, matrix products: 19.4 us -> none  [local(): jnp.einsum('tkij,tkjc->tic', weights[:, 0], picked, preferred_element_typ...]
    ppermute x8 -> x0, starting transfers between devices: 10.6 us -> none  [the longest x6 6.86 us: shifted(): lax.ppermute(value, axis, [(i, (i + by) % length) for i in range(length)])]
    unnamed x13 -> x1, local copies, waits for them, and re-layouts: 10.8 us -> 0.77 us
    concatenate x3 -> x0, other arithmetic: 3.35 us -> none  [the longest x1 3.29 us: extended(): value = jnp.concatenate([before, value, after], axis=dim)]
  transfers between devices with their start and end apart: 8 -> 0, of which waited for: 3 -> 0; matrix products, arithmetic and copies ran while one was open for 9% -> 0% of each run, Pallas kernels for 0% -> 0%
where the time goes in v1:
time: 147 us; the launch traced here: 146 us
  Pallas kernels  130 us (88%)
  other arithmetic  12.5 us (9%)
  local copies, waits for them, and re-layouts  2.24 us (2%)
    pallas_call x1, Pallas kernels, exchange(): pl.pallas_call(functools.partial(exchange_kernel, lats, lons, caps, bases...  82.7 us
    pallas_call x1, Pallas kernels, advect(): pl.pallas_call(functools.partial(advect_kernel, step_rows, slots), grid=(...  23.7 us
    pallas_call x1, Pallas kernels, share_needs(): pl.pallas_call(functools.partial(needs_kernel, lats, lons), out_shape=(ja...  14.2 us
    pallas_call x1, Pallas kernels, sum_over_devices(): pl.pallas_call(functools.partial(total_kernel, lats, lons), out_shape=jax...  9.71 us
    add x1, other arithmetic, local(): fixed = advected + (total[0] / total_area)[None, :, None]  4.9 us

profile of v1, /device:TPU:0, one launch (start us, length us, event | category | flops | bytes accessed | tf_op | source)
XLA Modules:
  0.0 145.8 jit_solution(3339021648189996356)
XLA Ops:
  0.0 0.8 copy.50
  0.8 0.1 sub.62
  0.9 0.7 fusion.20
  1.6 0.1 copy.49
  1.7 0.1 add.107
  1.7 0.7 iota_compare_fusion.4
  2.5 0.1 lt.59
  2.6 0.4 iota_compare_fusion.2
  3.0 0.6 fusion.25
  3.6 14.2 %share_needs.1 = (f32[32,8,128]{2,1,0:T(8,128)S(1)}, bf16[4,128,128]{2,1,0:T(8,128)(2,1)S(1)}, bf16[4,128,128]{2,1,0:T(8,128)(2,1)S(1)}) custom-call(f32[8,128]{1,0:T(8,128)} %get-tuple-element.196.need, bf16[64,128,128]{2,1,0:T(8,128)(2,1)} %bitcast.52), custom_call_target="tpu_custom_call" | custom-call | tf_op jit(solution)/shard_map/share_needs/pallas_call | solution.py:102
  17.8 0.8 dynamic_slice.6
  18.6 0.1 reduce_sum.63
  18.7 0.1 copy.51
  18.8 1.3 compare_reduce_fusion
  20.8 109.7 %conditional.1 = ((f32[64,128,128]{2,1,0:T(8,128)}, f32[8,128]{1,0:T(8,128)S(1)})) conditional(s32[]{:T(128)} %convert_element_type.37, (s32[64,8]{0,1:T(8,128)S(1)}, pred[64,8]{1,0:T(8,128)(4,1)S(1)}, f32[1024]{0:T(1024)S(1)}, f32[128,128]{1,0:T(8,128)S(1)}, f32[128,128]{1,0:T(8,128)S(1)}, /*index=5*/(), pred[1024,512]{1,0:T(8,128)(4,1)S(1)}, ...), branch_computations={%region_3.9_spmd, %region_9.11_spmd} | conditional | flops 2169510912 | bytes 214458368 | solution.py:403
  20.8 0.7 and_select_fusion
  21.4 0.1 select_reduce_fusion.2
  21.5 0.3 multiply_reduce_fusion
  21.9 0.8 select_reduce_fusion.1.lists
  22.7 0.0 copy-start.2
  22.7 0.0 copy-start
  22.7 0.0 copy-start.1
  22.7 82.7 %exchange.1.recv = bf16[206,128,128]{2,1,0:T(8,128)(2,1)} custom-call(s32[8,128]{1,0:T(8,128)} %select_reduce_fusion.1.lists, bf16[64,128,128]{2,1,0:T(8,128)(2,1)} %get-tuple-element.71.field, bf16[4,128,128]{2,1,0:T(8,128)(2,1)S(1)} %get-tuple-element.72.before, bf16[4,128,128]{2,1,0:T(8,128)(2,1)S(1)} %get-tuple-element.73.after), custom_call_target="tpu_custom_call" | custom-call | tf_op jit(solution)/shard_map/cond/branch_0_fun/exchange/pallas_call | solution.py:228
  105.5 0.0 copy-done.2
  105.5 0.1 add_bitcast_fusion
  105.5 0.4 select_reduce_fusion
  105.9 0.1 copy.52
  106.0 0.1 reshape.128
  106.1 0.1 reshape.129
  106.2 0.6 select_n.64.index
  106.8 0.0 copy-done
  106.8 0.0 copy-done.1
  106.8 23.7 %advect.1 = (f32[64,128,128]{2,1,0:T(8,128)}, f32[8,128]{1,0:T(8,128)S(1)}) custom-call(s32[512]{0:T(512)} %select_n.64.index, s32[64]{0:T(128)S(1)} %bitcast.57, f32[64]{0:T(128)S(1)} %get-tuple-element.69.area, bf16[64,1,8,128,128]{4,3,2,1,0:T(8,128)(2,1)} %get-tuple-element.70.weights, bf16[64,128,128]{2,1,0:T(8,128)(2,1)S(1)} %copy-done, ...), custom_call_target="tpu_custom_call" | custom-call | tf_op jit(solution)/shard_map/cond/branch_0_fun/advect/pallas_call | solution.py:296
  130.5 9.7 %sum_masses.1 = f32[8,128]{1,0:T(8,128)} custom-call(f32[8,128]{1,0:T(8,128)S(1)} %get-tuple-element.96.part), custom_call_target="tpu_custom_call" | custom-call | tf_op jit(solution)/shard_map/sum_masses/pallas_call | solution.py:129
  140.2 0.7 multiply_bitcast_fusion
  140.9 4.9 %broadcast_add_fusion = f32[64,128,128]{2,1,0:T(8,128)} fusion(f32[64,128,128]{2,1,0:T(8,128)} %get-tuple-element.95, f32[128]{0:T(128)S(1)} %multiply_bitcast_fusion), kind=kLoop, calls=%fused_computation.39 | loop fusion | flops 1048576 | bytes 8389120 | tf_op jit(solution)/shard_map/add | solution.py:405
  (8 shorter events, 0.1 us)
Async XLA Ops:
  22.7 82.8 %copy-start.2 = (s32[8]{0:T(128)S(1)}, s32[8]{0:T(128)}, u32[]{:S(2)}) copy-start(s32[8]{0:T(128)} %constant.109.clone.1) | copy-start | bytes 100 | tf_op jit(solution)/shard_map/cond
  22.7 84.1 %copy-start = (bf16[64,128,128]{2,1,0:T(8,128)(2,1)S(1)}, bf16[64,128,128]{2,1,0:T(8,128)(2,1)}, u32[]{:S(2)}) copy-start(bf16[64,128,128]{2,1,0:T(8,128)(2,1)} %get-tuple-element.71.field) | copy-start | bytes 6291460 | tf_op jit(solution)/shard_map/cond
  22.7 84.1 %copy-start.1 = (s32[64,1]{0,1:T(1,128)S(1)}, s32[64,1]{0,1:T(1,128)}, u32[]{:S(2)}) copy-start(s32[64,1]{0,1:T(1,128)} %get-tuple-element.68) | copy-start | bytes 772 | tf_op jit(solution)/shard_map/cond
